TPU v7x, 128 devices: a whole 4x4x4 slice. The times are simulated.
128 devices in a mesh: grp: 8 (over y_hi, z), pair: 16 (over x, y_lo, core).
Axes of the slice: x: 4, y: 4 (y_hi: 2, y_lo: 2; y = y_hi * 2 + y_lo), z: 4, core: 2. Of those that a mesh axis runs over, the one named last changes fastest.
Arguments:
- amplitudes: bfloat16 [128, 512, 512], P('pair', 'grp'), may hold values from -6 to 6
- cholesky: bfloat16 [512, 512, 2048], P('pair', 'grp'), may hold values from -0.09375 to 0.09375
Outputs:
- ladder_term: float32 [512, 4, 128], P('pair', None, 'grp')
All inputs are finite; a program needn't handle non-finite values.
Results may differ from a plain program's by a relative error of at most 0.003.
Values may be sent and summed in bfloat16 or wider, within the bound.
A program may use at most 128 MiB of HBM per device.

v0:
```python
import jax
import jax.numpy as jnp
from jax import lax
from jax.sharding import PartitionSpec as P

A_WIN = 4


def from_root(x, axis, root):
    return lax.dynamic_index_in_dim(lax.all_gather(x, axis), root, 0, keepdims=False)


def split_up(x, dim, length):
    before, after = (x.shape[:dim], x.shape[dim + 1 :])
    return jnp.moveaxis(x.reshape(*before, length, -1, *after), dim, 0)


def sent_and_summed(x, axis, dim):
    length = lax.axis_size(axis)
    blocks = lax.all_to_all(split_up(x, dim, length), axis, 0, 0, tiled=True)
    return jnp.sum(blocks, axis=0)


def build_tile(chol_local, portion):
    return lax.dot_general(
        chol_local, portion, (((2,), (2,)), ((), ())), preferred_element_type=jnp.float32
    ).astype(jnp.bfloat16)


def ladder(integrals, amp_part):
    return lax.dot_general(
        integrals, amp_part, (((1, 3), (1, 2)), ((), ())), preferred_element_type=jnp.float32
    )


def per_device(amplitudes, cholesky):
    own_window = cholesky[:A_WIN]
    everyone = lax.all_gather(amplitudes, "pair", axis=0, tiled=True)
    shared = from_root(own_window, "pair", 0)
    summed = ladder(
        build_tile(cholesky, lax.all_gather(shared, "grp", axis=1, tiled=True)), everyone
    )
    return sent_and_summed(summed, "grp", 2)


def solution(mesh):
    in_specs = (P("pair", "grp", None), P("pair", "grp", None))
    out_specs = P("pair", None, "grp")
    return jax.shard_map(
        per_device, mesh=mesh, in_specs=in_specs, out_specs=out_specs, check_vma=False
    )
```

profile of v0, /device:TPU:0, one launch (start us, length us, event | category | flops | bytes accessed | tf_op | source)
XLA Modules:
  0.0 334.3 jit_solution(7351327069050586795)
XLA Ops:
  6.5 0.0 all-gather.9.cloned.1.call-start
  6.5 2.4 slice.4
  8.9 0.0 all-gather.9.cloned.1.call-update
  8.9 0.0 all-gather.7.cloned.1.call-start
  9.0 2.1 copy.7
  11.1 0.0 all-gather.7.cloned.1.call-update
  11.1 0.0 all-gather.11.cloned.1.call-start
  11.2 91.9 %all-gather.9.cloned.1.call-done = bf16[64,64,2048]{2,1,0:T(8,128)(2,1)} async-done(((bf16[4,64,2048]{2,1,0:T(8,128)(2,1)}), bf16[64,64,2048]{2,1,0:T(8,128)(2,1)}) %all-gather.9.cloned.1.call-update) | async-done | bytes 16777232 | tf_op jit(solution)/shard_map/all_gather | solution.py:10
  103.1 2.4 slice.6
  105.5 0.0 all-gather.11.cloned.1.call-update
  105.5 52.1 %all-gather.7.cloned.1.call-done = bf16[128,64,512]{2,0,1:T(8,128)(2,1)} async-done(((bf16[8,64,512]{2,0,1:T(8,128)(2,1)}), bf16[128,64,512]{2,0,1:T(8,128)(2,1)}) %all-gather.7.cloned.1.call-update) | async-done | bytes 8388624 | tf_op jit(solution)/shard_map/all_gather | solution.py:38
  157.6 110.0 %all-gather.11.cloned.1.call-done = bf16[4,512,2048]{2,1,0:T(8,128)(2,1)} async-done(((bf16[4,64,2048]{2,1,0:T(8,128)(2,1)}), bf16[4,512,2048]{2,1,0:T(8,128)(2,1)}) %all-gather.11.cloned.1.call-update) | async-done | bytes 8388624 | tf_op jit(solution)/shard_map/all_gather | solution.py:41
  267.6 47.5 %fusion.2 = f32[32,4,128,1]{0,2,3,1:T(8,128)S(1)} fusion(bf16[128,64,512]{2,0,1:T(8,128)(2,1)} %all-gather.7.cloned.1.call-done, bf16[4,512,2048]{2,1,0:T(8,128)(2,1)} %all-gather.11.cloned.1.call-done, bf16[32,64,2048]{2,1,0:T(8,128)(2,1)} %param.3), kind=kOutput, calls=%fused_computation.2 | convolution fusion | flops 18257805312 | bytes 25231360 | tf_op jit(solution)/shard_map/dot_general | solution.py:31
  315.1 0.2 reshape.13
  315.3 10.4 %all_to_all.5 = f32[8,1,2048]{2,1,0:T(1,128)S(1)} all-to-all(f32[8,1,2048]{2,1,0:T(1,128)S(1)} %reshape.13), channel_id=1, replica_groups=mesh['grp'=8,'pair'=16] {'grp'}, dimensions={0} | all-to-all | bytes 131072 | tf_op jit(solution)/shard_map/all_to_all | solution.py:20
  325.7 0.5 broadcast
  326.2 0.8 reduce
  327.0 0.1 reshape.14
  327.1 0.6 bitcast_reduce_fusion
  (1 shorter events, 0.0 us)
Async XLA Ops:
  6.5 96.6 %all-gather.9.cloned.1.call-start = ((), (), s32[]{:S(2)}) async-start(), calls=%async_computation.2 | async-start | bytes 17825792 | tf_op jit(solution)/shard_map/all_gather | solution.py:10
  8.9 148.7 %all-gather.7.cloned.1.call-start = ((), (), s32[]{:S(2)}) async-start(), calls=%async_computation.1 | async-start | bytes 8912896 | tf_op jit(solution)/shard_map/all_gather | solution.py:38
  11.1 256.4 %all-gather.11.cloned.1.call-start = ((), (), s32[]{:S(2)}) async-start(), calls=%async_computation.3 | async-start | bytes 9437184 | tf_op jit(solution)/shard_map/all_gather | solution.py:41
Sparse Core Ops, SparseCore 0:
  9.1 94.0 all-gather.8
  104.8 52.8 all-gather.6
  159.9 107.6 all-gather.10
where the time goes:
time: 335 us; the launch traced here: 334 us
  waiting for transfers between devices  254 us (76%)
  matrix products  47.5 us (14%)
  between operations  13.1 us (4%)
  blocking collectives  10.4 us (3%)
  local copies, waits for them, and re-layouts  7.68 us (2%)
    all_gather x1, waiting for transfers between devices, per_device(): lax.all_gather(shared, 'grp', axis=1, tiled=True)  110 us
    all_gather x1, waiting for transfers between devices, from_root(): lax.all_gather(x, axis)  91.9 us
    all_gather x1, waiting for transfers between devices, per_device(): everyone = lax.all_gather(amplitudes, 'pair', axis=0, tiled=True)  52.1 us
    dot_general x1, matrix products, ladder(): lax.dot_general(integrals, amp_part, (((1, 3), (1, 2)), ((), ())), prefer...  47.5 us
    all_to_all x1, blocking collectives, sent_and_summed(): blocks = lax.all_to_all(split_up(x, dim, length), axis, 0, 0, tiled=True)  10.4 us
  transfers between devices with their start and end apart: 3, of which 3 were waited for; matrix products, arithmetic and copies ran while one was open for 1% of the time, Pallas kernels for 0%

commit v1 on v0

--- a/solution.py
+++ b/solution.py
@@ -35,7 +35,9 @@
 
 def per_device(amplitudes, cholesky):
     own_window = cholesky[:A_WIN]
-    everyone = lax.all_gather(amplitudes, "pair", axis=0, tiled=True)
+    everyone = jnp.concatenate(
+        lax.all_to_all(jnp.stack([amplitudes] * lax.axis_size("pair")), "pair", 0, 0), axis=0
+    )
     shared = from_root(own_window, "pair", 0)
     summed = ladder(
         build_tile(cholesky, lax.all_gather(shared, "grp", axis=1, tiled=True)), everyone

time: 335 us -> 368 us (1.099)
  waiting for transfers between devices: 254 us -> 271 us
  matrix products: 47.5 us -> 54.3 us
  starting transfers between devices: 0.09 us -> 5.06 us
    all_gather x1, waiting for transfers between devices: 110 us -> 176 us  [per_device(): lax.all_gather(shared, 'grp', axis=1, tiled=True)]
    all_gather x1 -> x0, waiting for transfers between devices: 52.1 us -> none  [per_device(): everyone = lax.all_gather(amplitudes, 'pair', axis=0, tiled=True)]
    dot_general x0 -> x1, matrix products: none -> 39.1 us  [build_tile(): lax.dot_general(chol_local, portion, (((2,), (2,)), ((), ())), preferred_...]
    dot_general x1, matrix products: 47.5 us -> 15.1 us  [ladder(): lax.dot_general(integrals, amp_part, (((1, 3), (1, 2)), ((), ())), prefer...]
    another operation x0 -> x1, local copies, waits for them, and re-layouts: none -> 5.32 us  [per_device(): jnp.stack([amplitudes] * lax.axis_size('pair'))]
    all_to_all x0 -> x1, starting transfers between devices: none -> 5.02 us  [per_device(): lax.all_to_all(jnp.stack([amplitudes] * lax.axis_size('pair')), 'pair', 0...]
  transfers between devices with their start and end apart: 3 -> 3, of which waited for: 3 -> 2; matrix products, arithmetic and copies ran while one was open for 1% -> 12% of each run, Pallas kernels for 0% -> 0%
where the time goes in v1:
time: 368 us; the launch traced here: 366 us
  waiting for transfers between devices  271 us (74%)
  matrix products  54.3 us (15%)
  between operations  13.4 us (4%)
  local copies, waits for them, and re-layouts  10.8 us (3%)
  blocking collectives  10.6 us (3%)
  starting transfers between devices  5.06 us (1%)
    all_gather x1, waiting for transfers between devices, per_device(): lax.all_gather(shared, 'grp', axis=1, tiled=True)  176 us
    all_gather x1, waiting for transfers between devices, from_root(): lax.all_gather(x, axis)  94.2 us
    dot_general x1, matrix products, build_tile(): lax.dot_general(chol_local, portion, (((2,), (2,)), ((), ())), preferred_...  39.1 us
    dot_general x1, matrix products, ladder(): lax.dot_general(integrals, amp_part, (((1, 3), (1, 2)), ((), ())), prefer...  15.1 us
    all_to_all x1, blocking collectives, sent_and_summed(): blocks = lax.all_to_all(split_up(x, dim, length), axis, 0, 0, tiled=True)  10.6 us
  transfers between devices with their start and end apart: 3, of which 2 were waited for; matrix products, arithmetic and copies ran while one was open for 12% of the time, Pallas kernels for 0%

profile of v1, /device:TPU:0, one launch (start us, length us, event | category | flops | bytes accessed | tf_op | source)
XLA Modules:
  0.0 366.2 jit_solution(12319157586844353387)
XLA Ops:
  6.5 0.0 all-gather.6.cloned.1.call-start
  6.5 2.3 slice.4
  8.8 0.0 all-gather.6.cloned.1.call-update
  8.9 0.0 all-gather.8.cloned.1.call-start
  8.9 94.2 %all-gather.6.cloned.1.call-done = bf16[64,64,2048]{2,1,0:T(8,128)(2,1)} async-done(((bf16[4,64,2048]{2,1,0:T(8,128)(2,1)}), bf16[64,64,2048]{2,1,0:T(8,128)(2,1)}) %all-gather.6.cloned.1.call-update) | async-done | bytes 16777232 | tf_op jit(solution)/shard_map/all_gather | solution.py:10
  103.1 2.4 slice.6
  105.5 0.0 all-gather.8.cloned.1.call-update
  105.5 5.3 %stack.2 = bf16[16,8,64,512]{3,2,1,0:T(8,128)(2,1)} broadcast(bf16[8,64,512]{2,1,0:T(8,128)(2,1)} %param.2), dimensions={1,2,3} | broadcast | bytes 8912896 | tf_op jit(solution)/shard_map/stack | solution.py:39
  110.8 5.0 %all-to-all-start = ((bf16[16,8,64,512]{3,2,1,0:T(8,128)(2,1)}), bf16[16,8,64,512]{3,2,1,0:T(8,128)(2,1)}, u32[]{:S(2)}, u32[]{:S(2)}) async-start(bf16[16,8,64,512]{3,2,1,0:T(8,128)(2,1)} %stack.2), calls=%async_computation | async-start | bytes 16777216 | tf_op jit(solution)/shard_map/all_to_all | solution.py:39
  115.8 176.4 %all-gather.8.cloned.1.call-done = bf16[4,512,2048]{2,1,0:T(8,128)(2,1)} async-done(((bf16[4,64,2048]{2,1,0:T(8,128)(2,1)}), bf16[4,512,2048]{2,1,0:T(8,128)(2,1)}) %all-gather.8.cloned.1.call-update) | async-done | bytes 8388624 | tf_op jit(solution)/shard_map/all_gather | solution.py:43
  292.2 39.1 %fusion.31 = bf16[32,64,4,512,1]{3,0,1,4,2:T(8,128)(2,1)} fusion(bf16[4,512,2048]{2,1,0:T(8,128)(2,1)} %all-gather.8.cloned.1.call-done, bf16[32,64,2048]{2,1,0:T(8,128)(2,1)} %param.3), kind=kOutput, calls=%fused_computation.1.clone.clone.clone.1 | convolution fusion | flops 17184063488 | bytes 25165824 | tf_op jit(solution)/shard_map/dot_general | solution.py:25
  331.4 0.0 all-to-all-done
  331.4 15.1 %fusion.9 = f32[8,32,4,16]{1,3,0,2:T(8,128)S(1)} fusion(bf16[8,16,64,512]{3,2,1,0:T(8,128)(2,1)} %bitcast.5, bf16[32,64,4,512,1]{3,0,1,4,2:T(8,128)(2,1)} %fusion.31), kind=kOutput, calls=%fused_computation.9 | convolution fusion | flops 1073741824 | bytes 16842752 | tf_op jit(solution)/shard_map/dot_general | solution.py:31
  346.5 0.2 reshape.16
  346.7 10.6 %all_to_all.10 = f32[8,1,2048]{2,1,0:T(1,128)S(1)} all-to-all(f32[8,1,2048]{2,1,0:T(1,128)S(1)} %reshape.16), channel_id=1, replica_groups=mesh['grp'=8,'pair'=16] {'grp'}, dimensions={0} | all-to-all | bytes 131072 | tf_op jit(solution)/shard_map/all_to_all | solution.py:20
  357.3 0.5 broadcast.2
  357.8 0.8 reduce
  358.6 0.1 reshape.17
  358.8 0.6 bitcast_reduce_fusion
  (1 shorter events, 0.0 us)
Async XLA Ops:
  6.5 96.6 %all-gather.6.cloned.1.call-start = ((), (), s32[]{:S(2)}) async-start(), calls=%async_computation.2 | async-start | bytes 17825792 | tf_op jit(solution)/shard_map/all_gather | solution.py:10
  8.9 283.4 %all-gather.8.cloned.1.call-start = ((), (), s32[]{:S(2)}) async-start(), calls=%async_computation.3 | async-start | bytes 9437184 | tf_op jit(solution)/shard_map/all_gather | solution.py:43
  110.8 220.6 %all-to-all-start = ((bf16[16,8,64,512]{3,2,1,0:T(8,128)(2,1)}), bf16[16,8,64,512]{3,2,1,0:T(8,128)(2,1)}, u32[]{:S(2)}, u32[]{:S(2)}) async-start(bf16[16,8,64,512]{3,2,1,0:T(8,128)(2,1)} %stack.2), calls=%async_computation | async-start | bytes 16777216 | tf_op jit(solution)/shard_map/all_to_all | solution.py:39
Sparse Core Ops, SparseCore 0:
  9.0 94.0 all-gather.5
  105.6 186.5 all-gather.7
